TPU v7x, 128 devices: a whole 4x4x4 slice. The times are simulated.
128 devices in a mesh: row: 16 (over x, y_lo, core), col: 8 (over y_hi, z).
Axes of the slice: x: 4, y: 4 (y_hi: 2, y_lo: 2; y = y_hi * 2 + y_lo), z: 4, core: 2. Of those that a mesh axis runs over, the one named last changes fastest.
Arguments:
- vectors: bfloat16 [64, 1024, 512], P('col', 'row'), may hold values from -6 to 6
- right_factors: bfloat16 [64, 64, 1024, 128], P('row', 'col'), may hold values from -0.1875 to 0.1875
- left_factors: bfloat16 [64, 64, 1024, 128], P('row', 'col'), may hold values from -0.09375 to 0.09375
- tile_ranks: int32 [64, 64], P('row', 'col'), may hold values from 16 to 128
- owner_map: int32 [64], replicated, may hold values from 0 to 63, as said below
Outputs:
- applied: bfloat16 [64, 1024, 512], P('row', 'col')
Inputs may be any that keep to these rules, and one draw needn't show every extreme that they name: owner_map is a permutation of 0 to 63; the 4 stored tile rows held by index i of row (stored rows i * 4 to i * 4 + 3) belong to 4 different indices of row of applied, i + c mod 16 for the same 4 offsets c at every i.
All inputs are finite; a program needn't handle non-finite values.
Results may differ from a plain program's by a relative error of at most 0.0066.
Values may be sent and summed in bfloat16 or wider, within the bound.
A program may use at most 128 MiB of HBM per device.

v0:
```python
import jax
import jax.numpy as jnp
from jax import lax
from jax.sharding import PartitionSpec as P


def split_up(x, dim, peers):
    before, after = (x.shape[:dim], x.shape[dim + 1 :])
    return jnp.moveaxis(x.reshape(*before, peers, -1, *after), dim, 0)


def sent_and_summed(x, axis, dim):
    pieces = split_up(x, dim, lax.axis_size(axis))
    arrived = lax.all_to_all(pieces, axis, split_axis=0, concat_axis=0, tiled=True)
    return arrived.astype(jnp.float32).sum(axis=0)


def masked_coeffs(products, tile_ranks, rank_width):
    columns = jnp.arange(rank_width, dtype=jnp.int32)
    kept_mask = columns[None, None, :] < tile_ranks[:, :, None]
    return jnp.where(kept_mask[:, :, :, None], products, 0.0).astype(jnp.bfloat16)


def build_buffer(payload, owner_map, cycle_size):
    held_rows = payload.shape[0]
    own_rows = lax.dynamic_slice_in_dim(owner_map, lax.axis_index("row") * held_rows, held_rows)
    target = own_rows // held_rows
    devices = jnp.arange(cycle_size, dtype=jnp.int32)
    matches = target[None, :] == devices[:, None]
    present = jnp.any(matches, axis=1)
    source_slot = jnp.sum(
        jnp.where(matches, jnp.arange(held_rows, dtype=jnp.int32)[None, :], 0), axis=1
    )
    picked = jnp.take(payload, source_slot, axis=0)
    return jnp.where(present[:, None, None], picked, jnp.zeros_like(picked))


def pick_rows(received, owner_map, held_rows):
    wanted = lax.axis_index("row") * held_rows + jnp.arange(held_rows, dtype=jnp.int32)
    matches = owner_map[None, :] == wanted[:, None]
    anchor = jnp.sum(
        jnp.where(matches, jnp.arange(owner_map.shape[0], dtype=jnp.int32)[None, :], 0), axis=1
    )
    return jnp.take(received, anchor // held_rows, axis=0)


def on_device(vectors, right_factors, left_factors, tile_ranks, owner_map):
    held_rows = right_factors.shape[0]
    rank_width = right_factors.shape[3]
    cycle_size = lax.axis_size("row")
    products = jnp.einsum(
        "ikbr,kbv->ikrv",
        right_factors,
        lax.all_gather(vectors, "row", axis=1, tiled=True),
        preferred_element_type=jnp.float32,
    )
    coeffs = masked_coeffs(products, tile_ranks, rank_width)
    partial_rows = jnp.einsum(
        "ikbr,ikrv->ibv", left_factors, coeffs, preferred_element_type=jnp.float32
    )
    summed = sent_and_summed(partial_rows.astype(jnp.bfloat16), "col", 1).astype(jnp.bfloat16)
    buffer = build_buffer(summed, owner_map, cycle_size)
    received = lax.all_to_all(buffer, "row", split_axis=0, concat_axis=0, tiled=True)
    applied = pick_rows(received, owner_map, held_rows)
    return applied


def solution(mesh):
    placed = (
        P("col", "row", None),
        P("row", "col", None, None),
        P("row", "col", None, None),
        P("row", "col"),
        P(),
    )
    return jax.shard_map(
        on_device, mesh=mesh, in_specs=placed, out_specs=P("row", "col", None), check_vma=False
    )
```

profile of v0, /device:TPU:25, one launch (start us, length us, event | category | flops | bytes accessed | tf_op | source)
XLA Modules:
  0.0 188.2 jit_solution(1948998117102520125)
XLA Ops:
  6.5 0.0 all-gather.2.cloned.1.call-start
  6.5 0.7 all-gather.2.cloned.1.call-update
  7.3 0.8 iota_compare_fusion
  8.0 55.5 %all-gather.2.cloned.1.call-done = bf16[8,1024,512]{2,1,0:T(8,128)(2,1)} async-done(((bf16[8,64,512]{2,1,0:T(8,128)(2,1)}), bf16[8,1024,512]{2,1,0:T(8,128)(2,1)}) %all-gather.2.cloned.1.call-update) | async-done | bytes 8388624 | tf_op jit(solution)/shard_map/all_gather | solution.py:54
  63.5 16.4 %fusion.5 = bf16[4,64,8,8,128]{4,3,2,1,0:T(8,128)(2,1)} fusion(bf16[4,8,1024,128]{3,2,1,0:T(8,128)(2,1)} %param.7, pred[4,8,128]{2,1,0:T(8,128)(4,1)S(1)} %iota_compare_fusion, bf16[4,8,1024,128]{3,2,1,0:T(8,128)(2,1)} %param.6, bf16[8,1024,512]{2,1,0:T(8,128)(2,1)} %all-gather.2.cloned.1.call-done), kind=kOutput, calls=%fused_computation.8 | convolution fusion | flops 8596226048 | bytes 29364224 | tf_op jit(solution)/shard_map/ikbr,ikrv->ibv/dot_general | solution.py:58
  79.9 5.3 %copy.18 = bf16[4,64,8,8,128]{4,3,1,0,2:T(8,128)(2,1)} copy(bf16[4,64,8,8,128]{4,3,2,1,0:T(8,128)(2,1)} %fusion.5) | data formatting | bytes 8388608 | tf_op jit(solution)/shard_map/reshape | solution.py:9
  85.2 0.0 copy-start
  85.2 7.0 %all-to-all-start = ((bf16[8,4,128,512]{2,3,1,0:T(8,128)(2,1)}), bf16[8,4,128,512]{2,3,1,0:T(8,128)(2,1)}, u32[]{:S(2)}, u32[]{:S(2)}) async-start(bf16[8,4,128,512]{2,3,1,0:T(8,128)(2,1)} %bitcast.48), calls=%async_computation | async-start | bytes 8388608 | tf_op jit(solution)/shard_map/all_to_all | solution.py:14
  92.1 0.0 copy-done
  92.1 0.1 and_select_fusion.1
  92.2 0.1 select_reduce_fusion
  92.3 0.1 fusion.16
  92.4 48.2 %all-to-all-done = bf16[8,4,128,512]{2,3,1,0:T(8,128)(2,1)} async-done(((bf16[8,4,128,512]{2,3,1,0:T(8,128)(2,1)}), bf16[8,4,128,512]{2,3,1,0:T(8,128)(2,1)}, u32[]{:S(2)}, u32[]{:S(2)}) %all-to-all-start) | async-done | bytes 4194336 | tf_op jit(solution)/shard_map/all_to_all | solution.py:14
  140.6 2.9 %reduce_sum.36 = bf16[4,128,512]{1,2,0:T(8,128)(2,1)S(1)} reduce(bf16[8,4,128,512]{2,3,1,0:T(8,128)(2,1)} %all-to-all-done, bf16[]{:T(256)} %constant.65.clone.1), dimensions={0}, to_apply=%region_3.4 | reduce | flops 1835008 | bytes 4718594 | tf_op jit(solution)/shard_map/reduce_sum | solution.py:15
  143.5 0.2 copy.13
  143.7 0.7 gather_fusion
  144.4 1.7 select_select_fusion
  146.1 5.8 %all-to-all-start.1 = ((bf16[16,128,512]{2,1,0:T(8,128)(2,1)}), bf16[16,128,512]{2,1,0:T(8,128)(2,1)S(1)}, u32[]{:S(2)}, u32[]{:S(2)}) async-start(bf16[16,128,512]{2,1,0:T(8,128)(2,1)} %select_select_fusion), calls=%async_computation.1 | async-start | bytes 4194304 | tf_op jit(solution)/shard_map/all_to_all | solution.py:63
  151.9 0.2 select_reduce_fusion.1
  152.1 27.7 %all-to-all-done.1 = bf16[16,128,512]{2,1,0:T(8,128)(2,1)S(1)} async-done(((bf16[16,128,512]{2,1,0:T(8,128)(2,1)}), bf16[16,128,512]{2,1,0:T(8,128)(2,1)S(1)}, u32[]{:S(2)}, u32[]{:S(2)}) %all-to-all-start.1) | async-done | bytes 2097184 | tf_op jit(solution)/shard_map/all_to_all | solution.py:63
  179.8 0.6 gather_fusion.1
  180.4 0.9 broadcast_select_fusion
  (7 shorter events, 0.1 us)
Async XLA Ops:
  6.5 57.0 %all-gather.2.cloned.1.call-start = ((), (), s32[]{:S(2)}) async-start(), calls=%async_computation.2 | async-start | bytes 8912896 | tf_op jit(solution)/shard_map/all_gather | solution.py:54
  85.2 7.0 %copy-start = (s32[64]{0:T(128)S(1)}, s32[64]{0:T(128)}, u32[]{:S(2)}) copy-start(s32[64]{0:T(128)} %param.9) | copy-start | bytes 772
  85.2 55.5 %all-to-all-start = ((bf16[8,4,128,512]{2,3,1,0:T(8,128)(2,1)}), bf16[8,4,128,512]{2,3,1,0:T(8,128)(2,1)}, u32[]{:S(2)}, u32[]{:S(2)}) async-start(bf16[8,4,128,512]{2,3,1,0:T(8,128)(2,1)} %bitcast.48), calls=%async_computation | async-start | bytes 8388608 | tf_op jit(solution)/shard_map/all_to_all | solution.py:14
  146.1 33.8 %all-to-all-start.1 = ((bf16[16,128,512]{2,1,0:T(8,128)(2,1)}), bf16[16,128,512]{2,1,0:T(8,128)(2,1)S(1)}, u32[]{:S(2)}, u32[]{:S(2)}) async-start(bf16[16,128,512]{2,1,0:T(8,128)(2,1)} %select_select_fusion), calls=%async_computation.1 | async-start | bytes 4194304 | tf_op jit(solution)/shard_map/all_to_all | solution.py:63
Sparse Core Ops, SparseCore 0:
  9.0 54.5 all-gather.1
where the time goes:
time: 189 us; the launch traced here: 188 us
  waiting for transfers between devices  132 us (70%)
  matrix products  16.4 us (9%)
  between operations  13.4 us (7%)
  starting transfers between devices  12.8 us (7%)
  local copies, waits for them, and re-layouts  6.76 us (4%)
  other arithmetic  6.68 us (4%)
    all_gather x1, waiting for transfers between devices, on_device(): lax.all_gather(vectors, 'row', axis=1, tiled=True)  55.5 us
    all_to_all x1, waiting for transfers between devices, sent_and_summed(): lax.all_to_all(pieces, axis, split_axis=0, concat_axis=0, tiled=True)  48.2 us
    all_to_all x1, waiting for transfers between devices, on_device(): lax.all_to_all(buffer, 'row', split_axis=0, concat_axis=0, tiled=True)  27.7 us
    dot_general x1, matrix products, on_device(): jnp.einsum('ikbr,ikrv->ibv', left_factors, coeffs, preferred_element_type...  16.4 us
    all_to_all x1, starting transfers between devices, sent_and_summed(): lax.all_to_all(pieces, axis, split_axis=0, concat_axis=0, tiled=True)  6.96 us
    all_to_all x1, starting transfers between devices, on_device(): lax.all_to_all(buffer, 'row', split_axis=0, concat_axis=0, tiled=True)  5.83 us
    reshape x1, local copies, waits for them, and re-layouts, split_up(): return jnp.moveaxis(x.reshape(*before, peers, -1, *after), dim, 0)  5.27 us
  transfers between devices with their start and end apart: 3, of which 3 were waited for; matrix products, arithmetic and copies ran while one was open for 1% of the time, Pallas kernels for 0%

commit v1 on v0

--- a/solution.py
+++ b/solution.py
@@ -51,7 +51,9 @@
     products = jnp.einsum(
         "ikbr,kbv->ikrv",
         right_factors,
-        lax.all_gather(vectors, "row", axis=1, tiled=True),
+        jnp.concatenate(
+            lax.all_to_all(jnp.stack([vectors] * lax.axis_size("row")), "row", 0, 0), axis=1
+        ),
         preferred_element_type=jnp.float32,
     )
     coeffs = masked_coeffs(products, tile_ranks, rank_width)

time: 189 us -> 271 us (1.43)
  waiting for transfers between devices: 132 us -> 199 us
  starting transfers between devices: 12.8 us -> 29.6 us
  between operations: 13.4 us -> 0.05 us
  local copies, waits for them, and re-layouts: 6.76 us -> 19.8 us
    all_to_all x0 -> x1, waiting for transfers between devices: none -> 123 us  [on_device(): lax.all_to_all(jnp.stack([vectors] * lax.axis_size('row')), 'row', 0, 0)]
    all_gather x1 -> x0, waiting for transfers between devices: 55.5 us -> none  [on_device(): lax.all_gather(vectors, 'row', axis=1, tiled=True)]
    all_to_all x1, starting transfers between devices: 5.83 us -> 15.7 us  [on_device(): lax.all_to_all(buffer, 'row', split_axis=0, concat_axis=0, tiled=True)]
    all_to_all x0 -> x1, local copies, waits for them, and re-layouts: none -> 7.71 us  [on_device(): lax.all_to_all(jnp.stack([vectors] * lax.axis_size('row')), 'row', 0, 0)]
    all_to_all x0 -> x1, starting transfers between devices: none -> 6.19 us  [on_device(): lax.all_to_all(jnp.stack([vectors] * lax.axis_size('row')), 'row', 0, 0)]
    another operation x0 -> x1, local copies, waits for them, and re-layouts: none -> 5.3 us  [on_device(): jnp.stack([vectors] * lax.axis_size('row'))]
  transfers between devices with their start and end apart: 3 -> 3, of which waited for: 3 -> 3; matrix products, arithmetic and copies ran while one was open for 1% -> 0% of each run, Pallas kernels for 0% -> 0%
where the time goes in v1:
time: 271 us; the launch traced here: 270 us
  waiting for transfers between devices  199 us (73%)
  starting transfers between devices  29.6 us (11%)
  local copies, waits for them, and re-layouts  19.8 us (7%)
  matrix products  16.3 us (6%)
  other arithmetic  6 us (2%)
    all_to_all x1, waiting for transfers between devices, on_device(): lax.all_to_all(jnp.stack([vectors] * lax.axis_size('row')), 'row', 0, 0)  123 us
    all_to_all x1, waiting for transfers between devices, sent_and_summed(): lax.all_to_all(pieces, axis, split_axis=0, concat_axis=0, tiled=True)  48.2 us
    all_to_all x1, waiting for transfers between devices, on_device(): lax.all_to_all(buffer, 'row', split_axis=0, concat_axis=0, tiled=True)  27.7 us
    dot_general x1, matrix products, on_device(): jnp.einsum('ikbr,ikrv->ibv', left_factors, coeffs, preferred_element_type...  16.3 us
    all_to_all x1, starting transfers between devices, on_device(): lax.all_to_all(buffer, 'row', split_axis=0, concat_axis=0, tiled=True)  15.7 us
    all_to_all x1, starting transfers between devices, sent_and_summed(): lax.all_to_all(pieces, axis, split_axis=0, concat_axis=0, tiled=True)  7.72 us
    all_to_all x1, local copies, waits for them, and re-layouts, on_device(): lax.all_to_all(jnp.stack([vectors] * lax.axis_size('row')), 'row', 0, 0)  7.71 us
    all_to_all x1, starting transfers between devices, on_device(): lax.all_to_all(jnp.stack([vectors] * lax.axis_size('row')), 'row', 0, 0)  6.19 us
  transfers between devices with their start and end apart: 3, of which 3 were waited for; matrix products, arithmetic and copies ran while one was open for 0% of the time, Pallas kernels for 0%

profile of v1, /device:TPU:25, one launch (start us, length us, event | category | flops | bytes accessed | tf_op | source)
XLA Modules:
  0.0 270.4 jit_solution(16064700066507868688)
XLA Ops:
  0.0 5.3 %stack.2 = bf16[16,8,64,512]{3,2,1,0:T(8,128)(2,1)} broadcast(bf16[8,64,512]{2,1,0:T(8,128)(2,1)} %param.5), dimensions={1,2,3} | broadcast | bytes 8912896 | tf_op jit(solution)/shard_map/stack | solution.py:55
  5.3 0.0 copy-start
  5.3 6.2 %all-to-all-start = ((bf16[16,8,64,512]{3,2,1,0:T(8,128)(2,1)}), bf16[16,8,64,512]{3,2,1,0:T(8,128)(2,1)}, u32[]{:S(2)}, u32[]{:S(2)}) async-start(bf16[16,8,64,512]{3,2,1,0:T(8,128)(2,1)} %stack.2), calls=%async_computation | async-start | bytes 16777216 | tf_op jit(solution)/shard_map/all_to_all | solution.py:55
  11.5 0.0 copy-done
  11.5 0.1 iota_compare_fusion
  11.6 122.7 %all-to-all-done = bf16[16,8,64,512]{3,2,1,0:T(8,128)(2,1)} async-done(((bf16[16,8,64,512]{3,2,1,0:T(8,128)(2,1)}), bf16[16,8,64,512]{3,2,1,0:T(8,128)(2,1)}, u32[]{:S(2)}, u32[]{:S(2)}) %all-to-all-start) | async-done | bytes 8388640 | tf_op jit(solution)/shard_map/all_to_all | solution.py:55
  134.3 7.7 %copy.15 = bf16[16,8,64,512]{3,2,0,1:T(8,128)(2,1)} copy(bf16[16,8,64,512]{3,2,1,0:T(8,128)(2,1)} %all-to-all-done) | data formatting | bytes 16777216 | tf_op jit(solution)/shard_map/all_to_all | solution.py:55
  142.0 16.3 %fusion.3 = bf16[4,64,8,8,128]{4,3,2,1,0:T(8,128)(2,1)} fusion(bf16[4,8,1024,128]{3,2,1,0:T(8,128)(2,1)} %param.7, pred[4,8,128]{2,1,0:T(8,128)(4,1)S(1)} %iota_compare_fusion, bf16[8,1024,512,1]{2,1,0,3:T(8,128)(2,1)} %bitcast.46, bf16[4,8,1024,128]{3,2,1,0:T(8,128)(2,1)} %param.6), kind=kOutput, calls=%fused_computation.6 | convolution fusion | flops 8596226048 | bytes 29364224 | tf_op jit(solution)/shard_map/ikbr,ikrv->ibv/dot_general | solution.py:60
  158.3 5.3 %copy.26 = bf16[4,64,8,8,128]{4,3,1,0,2:T(8,128)(2,1)} copy(bf16[4,64,8,8,128]{4,3,2,1,0:T(8,128)(2,1)} %fusion.3) | data formatting | bytes 8388608 | tf_op jit(solution)/shard_map/reshape | solution.py:9
  163.6 7.7 %all-to-all-start.1 = ((bf16[8,4,128,512]{2,3,1,0:T(8,128)(2,1)}), bf16[8,4,128,512]{2,3,1,0:T(8,128)(2,1)}, u32[]{:S(2)}, u32[]{:S(2)}) async-start(bf16[8,4,128,512]{2,3,1,0:T(8,128)(2,1)} %bitcast.45), calls=%async_computation.1 | async-start | bytes 8388608 | tf_op jit(solution)/shard_map/all_to_all | solution.py:14
  171.3 0.0 copy-done.1
  171.3 0.1 and_select_fusion.1
  171.4 0.1 select_reduce_fusion
  171.5 0.1 fusion.10
  171.6 48.2 %all-to-all-done.1 = bf16[8,4,128,512]{2,3,1,0:T(8,128)(2,1)} async-done(((bf16[8,4,128,512]{2,3,1,0:T(8,128)(2,1)}), bf16[8,4,128,512]{2,3,1,0:T(8,128)(2,1)}, u32[]{:S(2)}, u32[]{:S(2)}) %all-to-all-start.1) | async-done | bytes 4194336 | tf_op jit(solution)/shard_map/all_to_all | solution.py:14
  219.8 2.9 %reduce_sum.36 = bf16[4,128,512]{1,2,0:T(8,128)(2,1)S(1)} reduce(bf16[8,4,128,512]{2,3,1,0:T(8,128)(2,1)} %all-to-all-done.1, bf16[]{:T(256)} %constant.65.clone.1), dimensions={0}, to_apply=%region_3.4 | reduce | flops 1835008 | bytes 4718594 | tf_op jit(solution)/shard_map/reduce_sum | solution.py:15
  222.7 0.2 copy.19
  222.9 0.7 gather_fusion
  223.6 1.7 select_select_fusion
  225.2 15.7 %all-to-all-start.2 = ((bf16[16,128,512]{2,1,0:T(8,128)(2,1)}), bf16[16,128,512]{2,1,0:T(8,128)(2,1)S(1)}, u32[]{:S(2)}, u32[]{:S(2)}) async-start(bf16[16,128,512]{2,1,0:T(8,128)(2,1)} %select_select_fusion), calls=%async_computation.2 | async-start | bytes 4194304 | tf_op jit(solution)/shard_map/all_to_all | solution.py:65
  241.0 0.2 select_reduce_fusion.1
  241.2 27.7 %all-to-all-done.2 = bf16[16,128,512]{2,1,0:T(8,128)(2,1)S(1)} async-done(((bf16[16,128,512]{2,1,0:T(8,128)(2,1)}), bf16[16,128,512]{2,1,0:T(8,128)(2,1)S(1)}, u32[]{:S(2)}, u32[]{:S(2)}) %all-to-all-start.2) | async-done | bytes 2097184 | tf_op jit(solution)/shard_map/all_to_all | solution.py:65
  268.9 0.6 gather_fusion.1
  269.5 0.9 broadcast_select_fusion
  (8 shorter events, 0.1 us)
Async XLA Ops:
  5.3 6.2 %copy-start = (s32[4,8]{1,0:T(4,128)S(1)}, s32[4,8]{1,0:T(4,128)}, u32[]{:S(2)}) copy-start(s32[4,8]{1,0:T(4,128)} %param.8) | copy-start | bytes 388
  5.3 128.9 %all-to-all-start = ((bf16[16,8,64,512]{3,2,1,0:T(8,128)(2,1)}), bf16[16,8,64,512]{3,2,1,0:T(8,128)(2,1)}, u32[]{:S(2)}, u32[]{:S(2)}) async-start(bf16[16,8,64,512]{3,2,1,0:T(8,128)(2,1)} %stack.2), calls=%async_computation | async-start | bytes 16777216 | tf_op jit(solution)/shard_map/all_to_all | solution.py:55
  158.3 13.1 %copy-start.1 = (s32[64]{0:T(128)S(1)}, s32[64]{0:T(128)}, u32[]{:S(2)}) copy-start(s32[64]{0:T(128)} %param.9) | copy-start | bytes 772
  163.6 56.2 %all-to-all-start.1 = ((bf16[8,4,128,512]{2,3,1,0:T(8,128)(2,1)}), bf16[8,4,128,512]{2,3,1,0:T(8,128)(2,1)}, u32[]{:S(2)}, u32[]{:S(2)}) async-start(bf16[8,4,128,512]{2,3,1,0:T(8,128)(2,1)} %bitcast.45), calls=%async_computation.1 | async-start | bytes 8388608 | tf_op jit(solution)/shard_map/all_to_all | solution.py:14
  225.2 43.7 %all-to-all-start.2 = ((bf16[16,128,512]{2,1,0:T(8,128)(2,1)}), bf16[16,128,512]{2,1,0:T(8,128)(2,1)S(1)}, u32[]{:S(2)}, u32[]{:S(2)}) async-start(bf16[16,128,512]{2,1,0:T(8,128)(2,1)} %select_select_fusion), calls=%async_computation.2 | async-start | bytes 4194304 | tf_op jit(solution)/shard_map/all_to_all | solution.py:65
